TPU v7x, 32 devices: a whole 2x2x4 slice. The times are simulated.
32 devices in a mesh: row: 2 (over core), col: 8 (over z, x), grp: 2 (over y).
Axes of the slice: x: 2, y: 2, z: 4, core: 2. Of those that a mesh axis runs over, the one named last changes fastest.
Arguments:
- momentum: float32 [2, 4096, 16384], P('grp', 'row', 'col'), may hold values from -6 to 6
- gradient: bfloat16 [2, 4096, 16384], P('grp', 'row', 'col'), may hold values from -6 to 6
- factor_q: float32 [2, 16384, 256], P('grp', 'col', 'row'), may hold values from -0.046875 to 0.046875
- weights: float32 [2, 4096, 16384], P(None, 'row', ('col', 'grp')), may hold values from -6 to 6
- tokens: bfloat16 [256, 4096], P(None, 'row'), may hold values from -0.08984375 to 0.08984375
Outputs:
- momentum_out: float32 [2, 4096, 16384], P('grp', 'row', 'col')
- factor_out: float32 [2, 16384, 256], P('grp', 'col', 'row')
- weights_out: float32 [2, 4096, 16384], P(None, 'row', ('col', 'grp'))
- hidden: bfloat16 [256, 16384], P('row', ('col', 'grp'))
All inputs are finite; a program needn't handle non-finite values.
Results may differ from a plain program's by a relative error of at most 0.0061.
Values may be sent and summed in bfloat16 or wider, within the bound.
No kernel may reach another device: no remote copies, remote signals or barrier semaphores. Data moves between devices by JAX's collectives and lax.ppermute only.
A program may use at most 128 MiB of HBM per device.

v0:
```python
import math
import jax
import jax.numpy as jnp
from jax import lax
from jax.sharding import PartitionSpec as P

D = 4096
HID = 16384
feedback = 0.05
epsilon = 1e-06


def gram_of(left_rows):
    return jnp.dot(left_rows.T, left_rows, precision=lax.Precision.HIGHEST)


def orthonormal(gram_sum, left_rows):
    factor_l = jnp.linalg.cholesky(gram_sum)
    return jax.scipy.linalg.solve_triangular(factor_l, left_rows.T, lower=True).T


def local(momentum, gradient, factor_q, weights, tokens):
    buffer = momentum[0] + gradient[0].astype(jnp.float32)
    buffer_h = buffer.astype(jnp.bfloat16)
    partial_value = jnp.dot(
        buffer_h,
        lax.all_gather(factor_q[0].astype(jnp.bfloat16), "row", axis=1, tiled=True),
        preferred_element_type=jnp.float32,
    )
    left_full = lax.psum(partial_value, "col")
    gram_sum = lax.psum(gram_of(left_full), "row")
    left_h = orthonormal(gram_sum, left_full).astype(jnp.bfloat16)
    right_part = lax.dot_general(
        buffer_h, left_h, (((0,), (0,)), ((), ())), preferred_element_type=jnp.float32
    )
    rank_share = factor_q.shape[2]
    right_full = lax.psum(right_part, "row")
    squares = lax.psum(jnp.sum(right_full * right_full, axis=0), "col")
    new_q = right_full / jnp.sqrt(squares + epsilon)
    q_share = lax.dynamic_slice_in_dim(new_q, lax.axis_index("row") * rank_share, rank_share, 1)
    right_h = right_full.astype(jnp.bfloat16)
    new_q_h = new_q.astype(jnp.bfloat16)
    feedback_term = lax.dot_general(
        left_h, right_h, (((1,), (1,)), ((), ())), preferred_element_type=jnp.float32
    )
    mom_new = buffer - feedback * feedback_term
    left_both = lax.all_gather(left_h[None], "grp", axis=0, tiled=True)
    right_both = lax.all_to_all(new_q_h[None], "grp", split_axis=1, concat_axis=0, tiled=True)
    step_size = 0.4 * math.sqrt(max(D, HID))
    low_rank = lax.dot_general(
        left_both, right_both, (((2,), (2,)), ((0,), (0,))), preferred_element_type=jnp.float32
    )
    new_weights = weights - step_size * low_rank
    weights_h = new_weights.astype(jnp.bfloat16)
    dec_parts = lax.psum_scatter(
        jnp.einsum("bd,pdh->bph", tokens, weights_h, preferred_element_type=jnp.float32),
        "row",
        scatter_dimension=0,
        tiled=True,
    )
    hidden = (jax.nn.silu(dec_parts[:, 0]) * dec_parts[:, 1]).astype(jnp.bfloat16)
    return (mom_new[None], q_share[None], new_weights, hidden)


def solution(mesh):
    in_specs = (
        P("grp", "row", "col"),
        P("grp", "row", "col"),
        P("grp", "col", "row"),
        P(None, "row", ("col", "grp")),
        P(None, "row"),
    )
    out_specs = (
        P("grp", "row", "col"),
        P("grp", "col", "row"),
        P(None, "row", ("col", "grp")),
        P("row", ("col", "grp")),
    )
    return jax.shard_map(local, mesh=mesh, in_specs=in_specs, out_specs=out_specs, check_vma=False)
```

profile of v0, /device:TPU:0, one launch (start us, length us, event | category | flops | bytes accessed | tf_op | source)
XLA Modules:
  0.0 394.4 jit_solution(15597743867390131542)
XLA Ops:
  7.2 2.1 convert_element_type.31
  9.4 12.2 %all-gather.5.cloned.1.call-done = bf16[1,2048,256]{2,1,0:T(8,128)(2,1)} async-done(((bf16[1,2048,128]{2,1,0:T(8,128)(2,1)}), bf16[1,2048,256]{2,1,0:T(8,128)(2,1)}) %all-gather.5.cloned.1.call-update) | async-done | bytes 1048592 | tf_op jit(solution)/shard_map/all_gather | solution.py:27
  21.6 12.3 %fusion.9 = f32[2048,256]{1,0:T(8,128)} fusion(bf16[1,2048,256]{2,1,0:T(8,128)(2,1)} %all-gather.5.cloned.1.call-done, f32[1,2048,2048]{2,1,0:T(8,128)} %param.5, bf16[1,2048,2048]{2,1,0:T(8,128)(2,1)} %param.6), kind=kOutput, calls=%fused_computation.18 | convolution fusion | flops 2160066560 | bytes 28311552 | tf_op jit(solution)/shard_map/dot_general | solution.py:25
  34.0 103.6 %all-reduce.5.cloned.1.call-done = f32[2048,256]{1,0:T(8,128)} async-done(((f32[2048,256]{1,0:T(8,128)}), f32[2048,256]{1,0:T(8,128)}) %all-reduce.5.cloned.1.call-update) | async-done | bytes 2097168 | tf_op jit(solution)/shard_map/psum | solution.py:30
  137.6 6.4 %fusion.25 = f32[256,256]{0,1:T(8,128)} fusion(f32[2048,256]{1,0:T(8,128)} %all-reduce.5.cloned.1.call-done), kind=kOutput, calls=%fused_computation.56 | convolution fusion | flops 1610612736 | bytes 2359296 | tf_op jit(solution)/shard_map/dot_general | solution.py:14
  144.3 17.3 %all-reduce.7.cloned.1.call-done = f32[256,256]{0,1:T(8,128)} async-done(((f32[256,256]{0,1:T(8,128)}), f32[256,256]{0,1:T(8,128)}) %all-reduce.7.cloned.1.call-update) | async-done | bytes 262160 | tf_op jit(solution)/shard_map/psum | solution.py:31
  164.4 11.7 %cholesky.50 = f32[128,128]{1,0:T(8,128)S(1)} custom-call(f32[128,128]{1,0:T(8,128)S(1)} %cholesky.118), custom_call_target="Cholesky" | custom-call | tf_op jit(solution)/shard_map/jit(cholesky)/cholesky | solution.py:18
  176.2 9.8 %custom-call.15 = f32[1,128,128]{1,2,0:T(8,128)S(1)} custom-call(f32[1,128,128]{2,1,0:T(8,128)S(1)} %get-tuple-element.39), custom_call_target="InvertDiagBlocksLowerTriangular" | custom-call | tf_op jit(solution)/shard_map/jit(cholesky)/cholesky | solution.py:18
  188.2 11.7 %cholesky.105 = f32[128,128]{1,0:T(8,128)S(1)} custom-call(f32[128,128]{1,0:T(8,128)S(1)} %convolution_subtract_fusion.1), custom_call_target="Cholesky" | custom-call | tf_op jit(solution)/shard_map/jit(cholesky)/cholesky | solution.py:18
  203.0 5.7 %while.1 = (s32[]{:T(128)}, f32[256,256]{1,0:T(8,128)S(1)}, s32[2,2]{1,0:T(2,128)S(1)}, f32[2,128,128]{2,1,0:T(8,128)}, s32[]{:T(128)}) while((s32[]{:T(128)}, f32[256,256]{1,0:T(8,128)S(1)}, s32[2,2]{1,0:T(2,128)S(1)}, f32[2,128,128]{2,1,0:T(8,128)}, s32[]{:T(128)}) %tuple.32), condition=%wide.while_cond, body=%wide.while_body.sunk | while | flops 2 | bytes 132205 | solution.py:19
  204.1 2.0 bitcast_dynamic-update-slice_fusion.2
  206.7 2.0 bitcast_dynamic-update-slice_fusion.2
  208.8 20.5 %custom-call.16 = f32[2,128,128]{1,2,0:T(8,128)S(1)} custom-call(f32[2,128,128]{2,1,0:T(8,128)} %get-tuple-element.11), custom_call_target="InvertDiagBlocksLowerTriangular" | custom-call | tf_op jit(solution)/shard_map/jit(_solve_triangular)/triangular_solve | solution.py:19
  230.3 1.8 convolution_subtract_fusion
  233.3 13.1 %fusion.15 = f32[2048,256]{1,0:T(8,128)} fusion(bf16[128,2048]{1,0:T(8,128)(2,1)S(1)} %convolution_convert_fusion, bf16[128,2048]{1,0:T(8,128)(2,1)S(1)} %get-tuple-element.42, f32[1,2048,2048]{2,1,0:T(8,128)} %param.5, bf16[1,2048,2048]{2,1,0:T(8,128)(2,1)} %param.6), kind=kOutput, calls=%fused_computation.29 | convolution fusion | flops 2162163712 | bytes 28311552 | tf_op jit(solution)/shard_map/dot_general | solution.py:33
  248.5 20.6 %all-reduce.9.cloned.1.call-done = f32[2048,256]{1,0:T(8,128)} async-done(((f32[2048,256]{1,0:T(8,128)}), f32[2048,256]{1,0:T(8,128)}) %all-reduce.9.cloned.1.call-update) | async-done | bytes 2097168 | tf_op jit(solution)/shard_map/psum | solution.py:37
  269.1 2.0 multiply_reduce_fusion
  271.1 21.8 %psum.31 = f32[256]{0:T(256)S(1)} all-reduce(f32[256]{0:T(256)S(1)} %multiply_reduce_fusion), channel_id=1, replica_groups=mesh['row'=2,'col'=8,'grp'=2] {'col'}, use_global_device_ids=true, to_apply=%region_8.9 | all-reduce | flops 256 | bytes 2048 | tf_op jit(solution)/shard_map/psum | solution.py:38
  292.9 1.5 convert_bitcast_fusion
  294.4 12.9 %copy.33 = bf16[1,2048,256]{2,0,1:T(2,128)(2,1)} copy(bf16[1,2048,256]{2,1,0:T(8,128)(2,1)S(1)} %get-tuple-element.32) | data formatting | bytes 2097152 | tf_op jit(solution)/shard_map/broadcast_in_dim | solution.py:48
  307.8 12.6 %reduce.12 = bf16[2048,256]{1,0:T(8,128)(2,1)} reduce(bf16[2048,1,256]{2,1,0:T(2,128)(2,1)} %bitcast.81, bf16[]{:T(256)} %broadcast.117), dimensions={1}, to_apply=%bitcast.70.reduce_sub_computation | reduce | bytes 2097154
  320.5 2.2 reshape.56
  322.6 4.4 %all-to-all-start = ((bf16[2,2,131072]{2,1,0:T(2,128)(2,1)}), bf16[2,2,131072]{2,1,0:T(2,128)(2,1)}, u32[]{:S(2)}, u32[]{:S(2)}) async-start(bf16[2,2,131072]{2,1,0:T(2,128)(2,1)} %reshape.56), calls=%async_computation | async-start | bytes 2097152 | tf_op jit(solution)/shard_map/all_to_all | solution.py:48
  327.1 4.3 %copy.30 = bf16[4096,256]{1,0:T(8,128)(2,1)} copy(bf16[4096,256]{0,1:T(8,128)(2,1)} %all-gather.7.cloned.1.call-done) | data formatting | bytes 4194304 | tf_op jit(solution)/shard_map/all_gather | solution.py:47
  331.4 6.3 %all-to-all-done = bf16[2,2,131072]{2,1,0:T(2,128)(2,1)} async-done(((bf16[2,2,131072]{2,1,0:T(2,128)(2,1)}), bf16[2,2,131072]{2,1,0:T(2,128)(2,1)}, u32[]{:S(2)}, u32[]{:S(2)}) %all-to-all-start) | async-done | bytes 1048608 | tf_op jit(solution)/shard_map/all_to_all | solution.py:48
  337.7 3.0 reshape.57
  340.7 1.9 copy.31
  342.9 14.3 %multiply_subtract_fusion = f32[2,2048,1024]{2,1,0:T(8,128)} fusion(f32[2,2048,1024]{2,1,0:T(8,128)} %param.8, bf16[2,2048,256]{2,1,0:T(8,128)(2,1)S(1)} %bitcast.79, bf16[2,1024,256]{2,1,0:T(8,128)(2,1)S(1)} %bitcast.82), kind=kOutput, calls=%fused_computation.5 | convolution fusion | flops 2155872256 | bytes 36700160 | tf_op jit(solution)/shard_map/dot_general | solution.py:50
  357.2 9.6 %fusion.3 = f32[256,2,1024]{0,2,1:T(8,128)} fusion(f32[2,2048,1024]{2,1,0:T(8,128)} %multiply_subtract_fusion, bf16[256,2048]{1,0:T(8,128)(2,1)S(1)} %copy-done), kind=kOutput, calls=%fused_computation.12 | convolution fusion | flops 2151677952 | bytes 19922944 | tf_op jit(solution)/shard_map/bd,pdh->bph/dot_general | solution.py:56
  366.9 2.4 dynamic-slice_bitcast_fusion
  369.2 15.9 %fusion = f32[1,2048,2048]{2,1,0:T(8,128)} fusion(f32[1,2048,2048]{2,1,0:T(8,128)} %param.5, bf16[1,2048,2048]{2,1,0:T(8,128)(2,1)} %param.6, f32[2048,256]{1,0:T(8,128)S(1)} %copy-done.1, bf16[128,2048]{1,0:T(8,128)(2,1)S(1)} %copy-done.4, bf16[128,2048]{1,0:T(8,128)(2,1)S(1)} %copy-done.7), kind=kOutput, calls=%fused_computation.4 | convolution fusion | flops 2166882304 | bytes 45088768 | tf_op jit(solution)/shard_map/dot_general | solution.py:43
  385.1 1.3 fusion.13
  (59 shorter events, 14.5 us)
Async XLA Ops:
  7.2 350.1 %copy-start = (bf16[256,2048]{1,0:T(8,128)(2,1)S(1)}, bf16[256,2048]{1,0:T(8,128)(2,1)}, u32[]{:S(2)}) copy-start(bf16[256,2048]{1,0:T(8,128)(2,1)} %param.9) | copy-start | bytes 3145732
  7.2 14.5 %all-gather.5.cloned.1.call-start = ((), (), s32[]{:S(2)}) async-start(), calls=%async_computation.6 | async-start | bytes 1572864 | tf_op jit(solution)/shard_map/all_gather | solution.py:27
  9.4 128.2 %all-reduce.5.cloned.1.call-start = ((), (), s32[]{:S(2)}) async-start(), calls=%async_computation.2 | async-start | bytes 4194304 | tf_op jit(solution)/shard_map/psum | solution.py:30
  33.9 127.7 %all-reduce.7.cloned.1.call-start = ((), (), s32[]{:S(2)}) async-start(), calls=%async_computation.3 | async-start | bytes 524288 | tf_op jit(solution)/shard_map/psum | solution.py:31
  143.9 85.3 %copy-start.2 = (f32[2048,256]{1,0:T(8,128)S(1)}, f32[2048,256]{1,0:T(8,128)}, u32[]{:S(2)}) copy-start(f32[2048,256]{1,0:T(8,128)} %all-reduce.5.cloned.1.call-done) | copy-start | bytes 6291460
  144.0 125.1 %all-reduce.9.cloned.1.call-start = ((), (), s32[]{:S(2)}) async-start(), calls=%async_computation.4 | async-start | bytes 4194304 | tf_op jit(solution)/shard_map/psum | solution.py:37
  163.7 0.7 copy-start.10
  199.9 2.0 copy-start.9
  230.3 2.9 copy-start.5
  233.3 13.2 %copy-start.3 = (bf16[128,2048]{1,0:T(8,128)(2,1)}, bf16[128,2048]{1,0:T(8,128)(2,1)S(1)}, u32[]{:S(2)}) copy-start(bf16[128,2048]{1,0:T(8,128)(2,1)S(1)} %convolution_convert_fusion) | copy-start | bytes 1572868
  246.4 1.0 copy-start.6
  246.4 80.7 %all-gather.7.cloned.1.call-start = ((), (), s32[]{:S(2)}) async-start(), calls=%async_computation.7 | async-start | bytes 3145728 | tf_op jit(solution)/shard_map/all_gather | solution.py:47
  269.1 23.8 %copy-start.1 = (f32[2048,256]{1,0:T(8,128)S(1)}, f32[2048,256]{1,0:T(8,128)}, u32[]{:S(2)}) copy-start(f32[2048,256]{1,0:T(8,128)} %all-reduce.9.cloned.1.call-done) | copy-start | bytes 6291460
  322.6 15.1 %all-to-all-start = ((bf16[2,2,131072]{2,1,0:T(2,128)(2,1)}), bf16[2,2,131072]{2,1,0:T(2,128)(2,1)}, u32[]{:S(2)}, u32[]{:S(2)}) async-start(bf16[2,2,131072]{2,1,0:T(2,128)(2,1)} %reshape.56), calls=%async_computation | async-start | bytes 2097152 | tf_op jit(solution)/shard_map/all_to_all | solution.py:48
  327.1 58.0 %reduce-scatter.2.cloned.1.call-start = ((), (), s32[]{:S(2)}) async-start(), calls=%async_computation.5 | async-start | bytes 3145728 | tf_op jit(solution)/shard_map/reduce_scatter | solution.py:55
  340.7 2.2 copy-start.8
  366.8 2.4 copy-start.4
  366.9 2.4 copy-start.7
Sparse Core Ops, SparseCore 0:
  10.1 11.4 all-gather.4
  34.0 103.4 all-reduce.4
  144.1 17.4 all-reduce.6
  246.5 22.4 all-reduce.8
  271.0 34.2 all-gather.6
  367.0 5.6 reduce-scatter.1
where the time goes:
time: 400 us; the launch traced here: 394 us
  waiting for transfers between devices  160 us (40%)
  matrix products  77.6 us (19%)
  other arithmetic  77.2 us (19%)
  local copies, waits for them, and re-layouts  36.3 us (9%)
  blocking collectives  21.8 us (5%)
  between operations  15.9 us (4%)
  starting transfers between devices  4.96 us (1%)
    psum x1, waiting for transfers between devices, local(): left_full = lax.psum(partial_value, 'col')  104 us
    another operation x6, other arithmetic, orthonormal(): factor_l = jnp.linalg.cholesky(gram_sum)  34 us
    psum x1, blocking collectives, local(): squares = lax.psum(jnp.sum(right_full * right_full, axis=0), 'col')  21.8 us
    another operation x3, other arithmetic, orthonormal(): jax.scipy.linalg.solve_triangular(factor_l, left_rows.T, lower=True)  21.5 us
    psum x1, waiting for transfers between devices, local(): right_full = lax.psum(right_part, 'row')  20.6 us
    psum x1, waiting for transfers between devices, local(): gram_sum = lax.psum(gram_of(left_full), 'row')  17.3 us
    dot_general x1, matrix products, local(): lax.dot_general(left_h, right_h, (((1,), (1,)), ((), ())), preferred_elem...  15.9 us
    dot_general x1, matrix products, local(): lax.dot_general(left_both, right_both, (((2,), (2,)), ((0,), (0,))), pref...  14.3 us
  transfers between devices with their start and end apart: 7, of which 5 were waited for; matrix products, arithmetic and copies ran while one was open for 14% of the time, Pallas kernels for 0%

commit v1 on v0

--- a/solution.py
+++ b/solution.py
@@ -27,7 +27,11 @@
         lax.all_gather(factor_q[0].astype(jnp.bfloat16), "row", axis=1, tiled=True),
         preferred_element_type=jnp.float32,
     )
-    left_full = lax.psum(partial_value, "col")
+    left_full = partial_value
+    for hop in (1, 2, 4):
+        left_full = left_full + lax.ppermute(
+            left_full, "col", [(dev, dev ^ hop) for dev in range(8)]
+        )
     gram_sum = lax.psum(gram_of(left_full), "row")
     left_h = orthonormal(gram_sum, left_full).astype(jnp.bfloat16)
     right_part = lax.dot_general(

time: 400 us -> 480 us (1.20)
  waiting for transfers between devices: 160 us -> 236 us
  starting transfers between devices: 4.96 us -> 11.5 us
    ppermute x0 -> x3, waiting for transfers between devices: none -> 181 us  [local(): lax.ppermute(left_full, 'col', [(dev, dev ^ hop) for dev in range(8)])]
    psum x1 -> x0, waiting for transfers between devices: 104 us -> none  [local(): left_full = lax.psum(partial_value, 'col')]
    ppermute x0 -> x3, starting transfers between devices: none -> 6.38 us  [local(): lax.ppermute(left_full, 'col', [(dev, dev ^ hop) for dev in range(8)])]
    unnamed x27 -> x21, local copies, waits for them, and re-layouts: 10.4 us -> 8.77 us
  transfers between devices with their start and end apart: 7 -> 9, of which waited for: 5 -> 7; matrix products, arithmetic and copies ran while one was open for 14% -> 12% of each run, Pallas kernels for 0% -> 0%
where the time goes in v1:
time: 480 us; the launch traced here: 474 us
  waiting for transfers between devices  236 us (49%)
  other arithmetic  79.1 us (16%)
  matrix products  76.2 us (16%)
  local copies, waits for them, and re-layouts  33.5 us (7%)
  blocking collectives  21.8 us (5%)
  between operations  15.6 us (3%)
  starting transfers between devices  11.5 us (2%)
    ppermute x3, waiting for transfers between devices, local(): lax.ppermute(left_full, 'col', [(dev, dev ^ hop) for dev in range(8)])  181 us
    another operation x6, other arithmetic, orthonormal(): factor_l = jnp.linalg.cholesky(gram_sum)  33.9 us
    psum x1, blocking collectives, local(): squares = lax.psum(jnp.sum(right_full * right_full, axis=0), 'col')  21.8 us
    psum x1, waiting for transfers between devices, local(): right_full = lax.psum(right_part, 'row')  21.5 us
    another operation x3, other arithmetic, orthonormal(): jax.scipy.linalg.solve_triangular(factor_l, left_rows.T, lower=True)  19.7 us
    dot_general x1, matrix products, local(): lax.dot_general(left_h, right_h, (((1,), (1,)), ((), ())), preferred_elem...  15.9 us
    psum x1, waiting for transfers between devices, local(): gram_sum = lax.psum(gram_of(left_full), 'row')  15.8 us
    dot_general x1, matrix products, local(): lax.dot_general(left_both, right_both, (((2,), (2,)), ((0,), (0,))), pref...  14.3 us
  transfers between devices with their start and end apart: 9, of which 7 were waited for; matrix products, arithmetic and copies ran while one was open for 12% of the time, Pallas kernels for 0%

profile of v1, /device:TPU:0, one launch (start us, length us, event | category | flops | bytes accessed | tf_op | source)
XLA Modules:
  0.0 474.3 jit_solution(14305211493571445727)
XLA Ops:
  7.2 2.1 convert_element_type.31
  9.4 12.2 %all-gather.5.cloned.1.call-done = bf16[1,2048,256]{2,1,0:T(8,128)(2,1)} async-done(((bf16[1,2048,128]{2,1,0:T(8,128)(2,1)}), bf16[1,2048,256]{2,1,0:T(8,128)(2,1)}) %all-gather.5.cloned.1.call-update) | async-done | bytes 1048592 | tf_op jit(solution)/shard_map/all_gather | solution.py:27
  21.6 11.1 %fusion.9 = f32[2048,256]{1,0:T(8,128)S(1)} fusion(bf16[1,2048,256]{2,1,0:T(8,128)(2,1)} %all-gather.5.cloned.1.call-done, f32[1,2048,2048]{2,1,0:T(8,128)} %param.5, bf16[1,2048,2048]{2,1,0:T(8,128)(2,1)} %param.6), kind=kOutput, calls=%fused_computation.18 | convolution fusion | flops 2160066560 | bytes 28311552 | tf_op jit(solution)/shard_map/dot_general | solution.py:25
  34.6 46.1 %collective-permute-done = f32[2048,256]{1,0:T(8,128)S(1)} collective-permute-done((f32[2048,256]{1,0:T(8,128)S(1)}, f32[2048,256]{1,0:T(8,128)S(1)}, u32[]{:S(2)}, u32[]{:S(2)}) %collective-permute-start) | collective-permute-done | bytes 2097184 | tf_op jit(solution)/shard_map/ppermute | solution.py:32
  82.7 45.2 %collective-permute-done.1 = f32[2048,256]{1,0:T(8,128)S(1)} collective-permute-done((f32[2048,256]{1,0:T(8,128)S(1)}, f32[2048,256]{1,0:T(8,128)S(1)}, u32[]{:S(2)}, u32[]{:S(2)}) %collective-permute-start.1) | collective-permute-done | bytes 2097184 | tf_op jit(solution)/shard_map/ppermute | solution.py:32
  128.2 2.7 collective-permute-start.2
  130.9 89.4 %collective-permute-done.2 = f32[2048,256]{1,0:T(8,128)} collective-permute-done((f32[2048,256]{1,0:T(8,128)S(1)}, f32[2048,256]{1,0:T(8,128)}, u32[]{:S(2)}, u32[]{:S(2)}) %collective-permute-start.2) | collective-permute-done | bytes 2097184 | tf_op jit(solution)/shard_map/ppermute | solution.py:32
  220.3 6.4 %fusion.12 = f32[256,256]{0,1:T(8,128)} fusion(f32[2048,256]{1,0:T(8,128)S(1)} %add.62, f32[2048,256]{1,0:T(8,128)} %collective-permute-done.2), kind=kOutput, calls=%fused_computation.25 | convolution fusion | flops 1611137024 | bytes 4456448 | tf_op jit(solution)/shard_map/dot_general | solution.py:14
  227.3 3.2 add_bitcast_fusion
  230.4 15.8 %all-reduce.4.cloned.1.call-done = f32[256,256]{0,1:T(8,128)} async-done(((f32[256,256]{0,1:T(8,128)}), f32[256,256]{0,1:T(8,128)}) %all-reduce.4.cloned.1.call-update) | async-done | bytes 262160 | tf_op jit(solution)/shard_map/psum | solution.py:35
  248.3 11.7 %cholesky.50 = f32[128,128]{1,0:T(8,128)S(1)} custom-call(f32[128,128]{1,0:T(8,128)S(1)} %cholesky.118), custom_call_target="Cholesky" | custom-call | tf_op jit(solution)/shard_map/jit(cholesky)/cholesky | solution.py:18
  260.1 9.8 %custom-call.15 = f32[1,128,128]{1,2,0:T(8,128)S(1)} custom-call(f32[1,128,128]{2,1,0:T(8,128)S(1)} %get-tuple-element.39), custom_call_target="InvertDiagBlocksLowerTriangular" | custom-call | tf_op jit(solution)/shard_map/jit(cholesky)/cholesky | solution.py:18
  270.4 11.7 %cholesky.105 = f32[128,128]{1,0:T(8,128)S(1)} custom-call(f32[128,128]{1,0:T(8,128)S(1)} %convolution_subtract_fusion), custom_call_target="Cholesky" | custom-call | tf_op jit(solution)/shard_map/jit(cholesky)/cholesky | solution.py:18
  284.2 4.2 while.1
  288.4 19.7 %custom-call.16 = f32[2,128,128]{1,2,0:T(8,128)S(1)} custom-call(f32[2,128,128]{2,1,0:T(8,128)S(1)} %get-tuple-element.11), custom_call_target="InvertDiagBlocksLowerTriangular" | custom-call | tf_op jit(solution)/shard_map/jit(_solve_triangular)/triangular_solve | solution.py:19
  308.1 2.4 fusion.27
  313.4 13.1 %fusion.17 = f32[2048,256]{1,0:T(8,128)} fusion(bf16[128,2048]{1,0:T(8,128)(2,1)S(1)} %convolution_convert_fusion, bf16[128,2048]{1,0:T(8,128)(2,1)S(1)} %get-tuple-element.42, f32[1,2048,2048]{2,1,0:T(8,128)} %param.5, bf16[1,2048,2048]{2,1,0:T(8,128)(2,1)} %param.6), kind=kOutput, calls=%fused_computation.32 | convolution fusion | flops 2162163712 | bytes 28311552 | tf_op jit(solution)/shard_map/dot_general | solution.py:37
  327.7 21.5 %all-reduce.6.cloned.1.call-done = f32[2048,256]{1,0:T(8,128)} async-done(((f32[2048,256]{1,0:T(8,128)}), f32[2048,256]{1,0:T(8,128)}) %all-reduce.6.cloned.1.call-update) | async-done | bytes 2097168 | tf_op jit(solution)/shard_map/psum | solution.py:41
  349.2 2.0 multiply_reduce_fusion
  351.2 21.8 %psum.23 = f32[256]{0:T(256)S(1)} all-reduce(f32[256]{0:T(256)S(1)} %multiply_reduce_fusion), channel_id=1, replica_groups=mesh['row'=2,'col'=8,'grp'=2] {'col'}, use_global_device_ids=true, to_apply=%region_7.8 | all-reduce | flops 256 | bytes 2048 | tf_op jit(solution)/shard_map/psum | solution.py:42
  374.6 12.9 %copy.33 = bf16[1,2048,256]{2,0,1:T(2,128)(2,1)} copy(bf16[1,2048,256]{2,1,0:T(8,128)(2,1)S(1)} %get-tuple-element.32) | data formatting | bytes 2097152 | tf_op jit(solution)/shard_map/broadcast_in_dim | solution.py:52
  388.0 12.6 %reduce.12 = bf16[2048,256]{1,0:T(8,128)(2,1)} reduce(bf16[2048,1,256]{2,1,0:T(2,128)(2,1)} %bitcast.77, bf16[]{:T(256)} %broadcast.117), dimensions={1}, to_apply=%bitcast.68.reduce_sub_computation | reduce | bytes 2097154
  400.6 2.2 reshape.56
  402.8 4.4 all-to-all-start
  407.3 4.3 copy.30
  411.6 6.2 %all-to-all-done = bf16[2,2,131072]{2,1,0:T(2,128)(2,1)} async-done(((bf16[2,2,131072]{2,1,0:T(2,128)(2,1)}), bf16[2,2,131072]{2,1,0:T(2,128)(2,1)}, u32[]{:S(2)}, u32[]{:S(2)}) %all-to-all-start) | async-done | bytes 1048608 | tf_op jit(solution)/shard_map/all_to_all | solution.py:52
  417.9 3.0 reshape.57
  420.9 1.9 copy.31
  423.1 14.3 %multiply_subtract_fusion = f32[2,2048,1024]{2,1,0:T(8,128)} fusion(f32[2,2048,1024]{2,1,0:T(8,128)} %param.8, bf16[2,2048,256]{2,1,0:T(8,128)(2,1)S(1)} %bitcast.75, bf16[2,1024,256]{2,1,0:T(8,128)(2,1)S(1)} %bitcast.78), kind=kOutput, calls=%fused_computation.5 | convolution fusion | flops 2155872256 | bytes 36700160 | tf_op jit(solution)/shard_map/dot_general | solution.py:54
  437.4 9.6 %fusion.3 = f32[256,2,1024]{0,2,1:T(8,128)} fusion(f32[2,2048,1024]{2,1,0:T(8,128)} %multiply_subtract_fusion, bf16[256,2048]{1,0:T(8,128)(2,1)S(1)} %copy-done), kind=kOutput, calls=%fused_computation.11 | convolution fusion | flops 2151677952 | bytes 19922944 | tf_op jit(solution)/shard_map/bd,pdh->bph/dot_general | solution.py:60
  447.0 2.4 dynamic-slice_bitcast_fusion
  449.4 15.9 %fusion = f32[1,2048,2048]{2,1,0:T(8,128)} fusion(f32[1,2048,2048]{2,1,0:T(8,128)} %param.5, bf16[1,2048,2048]{2,1,0:T(8,128)(2,1)} %param.6, f32[2048,256]{1,0:T(8,128)S(1)} %copy-done.1, bf16[128,2048]{1,0:T(8,128)(2,1)S(1)} %copy-done.5, bf16[128,2048]{1,0:T(8,128)(2,1)S(1)} %copy-done.3), kind=kOutput, calls=%fused_computation.4 | convolution fusion | flops 2166882304 | bytes 45088768 | tf_op jit(solution)/shard_map/dot_general | solution.py:47
  (59 shorter events, 20.8 us)
Async XLA Ops:
  7.2 430.2 %copy-start = (bf16[256,2048]{1,0:T(8,128)(2,1)S(1)}, bf16[256,2048]{1,0:T(8,128)(2,1)}, u32[]{:S(2)}) copy-start(bf16[256,2048]{1,0:T(8,128)(2,1)} %param.9) | copy-start | bytes 3145732
  7.2 14.5 %all-gather.5.cloned.1.call-start = ((), (), s32[]{:S(2)}) async-start(), calls=%async_computation.5 | async-start | bytes 1572864 | tf_op jit(solution)/shard_map/all_gather | solution.py:27
  9.4 236.8 %all-reduce.4.cloned.1.call-start = ((), (), s32[]{:S(2)}) async-start(), calls=%async_computation.2 | async-start | bytes 524288 | tf_op jit(solution)/shard_map/psum | solution.py:35
  32.7 47.9 %collective-permute-start = (f32[2048,256]{1,0:T(8,128)S(1)}, f32[2048,256]{1,0:T(8,128)S(1)}, u32[]{:S(2)}, u32[]{:S(2)}) collective-permute-start(f32[2048,256]{1,0:T(8,128)S(1)} %fusion.9), channel_id=1, source_target_pairs={{0,2},{2,0},{4,6},{6,4},{8,10},{10,8},{12,14},{14,12},{1,3},{3,1},... | collective-permute-start | bytes 6291464 | tf_op jit(solution)/shard_map/ppermute | solution.py:32
  80.9 47.0 %collective-permute-start.1 = (f32[2048,256]{1,0:T(8,128)S(1)}, f32[2048,256]{1,0:T(8,128)S(1)}, u32[]{:S(2)}, u32[]{:S(2)}) collective-permute-start(f32[2048,256]{1,0:T(8,128)S(1)} %add.61), channel_id=1, source_target_pairs={{0,4},{2,6},{4,0},{6,2},{8,12},{10,14},{12,8},{14,10},{1,5},{3,7},... | collective-permute-start | bytes 6291464 | tf_op jit(solution)/shard_map/ppermute | solution.py:32
  128.2 92.1 %collective-permute-start.2 = (f32[2048,256]{1,0:T(8,128)S(1)}, f32[2048,256]{1,0:T(8,128)}, u32[]{:S(2)}, u32[]{:S(2)}) collective-permute-start(f32[2048,256]{1,0:T(8,128)S(1)} %add.62), channel_id=1, source_target_pairs={{0,8},{2,10},{4,12},{6,14},{8,0},{10,2},{12,4},{14,6},{1,9},{3,11}... | collective-permute-start | bytes 6291464 | tf_op jit(solution)/shard_map/ppermute | solution.py:32
  226.7 122.4 %all-reduce.6.cloned.1.call-start = ((), (), s32[]{:S(2)}) async-start(), calls=%async_computation.3 | async-start | bytes 4194304 | tf_op jit(solution)/shard_map/psum | solution.py:41
  308.0 4.3 copy-start.7
  310.5 16.1 %copy-start.2 = (bf16[128,2048]{1,0:T(8,128)(2,1)}, bf16[128,2048]{1,0:T(8,128)(2,1)S(1)}, u32[]{:S(2)}) copy-start(bf16[128,2048]{1,0:T(8,128)(2,1)S(1)} %get-tuple-element.42) | copy-start | bytes 1572868
  313.4 13.2 %copy-start.4 = (bf16[128,2048]{1,0:T(8,128)(2,1)}, bf16[128,2048]{1,0:T(8,128)(2,1)S(1)}, u32[]{:S(2)}) copy-start(bf16[128,2048]{1,0:T(8,128)(2,1)S(1)} %convolution_convert_fusion) | copy-start | bytes 1572868
  326.5 80.8 %all-gather.7.cloned.1.call-start = ((), (), s32[]{:S(2)}) async-start(), calls=%async_computation.6 | async-start | bytes 3145728 | tf_op jit(solution)/shard_map/all_gather | solution.py:51
  349.2 23.9 %copy-start.1 = (f32[2048,256]{1,0:T(8,128)S(1)}, f32[2048,256]{1,0:T(8,128)}, u32[]{:S(2)}) copy-start(f32[2048,256]{1,0:T(8,128)} %all-reduce.6.cloned.1.call-done) | copy-start | bytes 6291460
  402.8 15.1 %all-to-all-start = ((bf16[2,2,131072]{2,1,0:T(2,128)(2,1)}), bf16[2,2,131072]{2,1,0:T(2,128)(2,1)}, u32[]{:S(2)}, u32[]{:S(2)}) async-start(bf16[2,2,131072]{2,1,0:T(2,128)(2,1)} %reshape.56), calls=%async_computation | async-start | bytes 2097152 | tf_op jit(solution)/shard_map/all_to_all | solution.py:52
  407.2 58.0 %reduce-scatter.2.cloned.1.call-start = ((), (), s32[]{:S(2)}) async-start(), calls=%async_computation.4 | async-start | bytes 3145728 | tf_op jit(solution)/shard_map/reduce_scatter | solution.py:59
  420.9 2.2 copy-start.6
  447.0 2.4 copy-start.3
  447.0 2.4 copy-start.5
Sparse Core Ops, SparseCore 0:
  10.1 11.4 all-gather.4
  226.9 19.3 all-reduce.3
  326.7 22.4 all-reduce.5
  351.2 34.2 all-gather.6
  447.1 5.6 reduce-scatter.1
